TPU v7x, 256 devices: a whole 4x4x8 slice. The times are simulated.
256 devices in a mesh: row: 8 (over y, x_lo), col: 16 (over z, core), layer: 2 (over x_hi).
Axes of the slice: x: 4 (x_hi: 2, x_lo: 2; x = x_hi * 2 + x_lo), y: 4, z: 8, core: 2. Of those that a mesh axis runs over, the one named last changes fastest.
Arguments:
- tokens: bfloat16 [10240, 8192], P('row', 'col'), may hold values from -6 to 6
- up_weight: bfloat16 [8192, 16384], P('row', 'col'), may hold values from -0.0625 to 0.0625
Outputs:
- up: bfloat16 [10240, 16384], P('row', ('col', 'layer'))
All inputs are finite; a program needn't handle non-finite values.
Results may differ from a plain program's by a relative error of at most 0.001.
Values may be sent and summed in bfloat16 or wider, within the bound.
No kernel may reach another device: no remote copies, remote signals or barrier semaphores. Data moves between devices by JAX's collectives and lax.ppermute only.
A program may use at most 128 MiB of HBM per device.

v0:
```python
import jax
import jax.numpy as jnp
from jax import lax
from jax.experimental import pallas as pl
from jax.experimental.pallas import tpu as pltpu
from jax.sharding import Mesh
from jax.sharding import PartitionSpec as P


AXES = ("y", "xl", "z", "core", "xh")


def ring(size, shift):
    return [(i, (i + shift) % size) for i in range(size)]


def block_product(counts, a, b, c, c_rows, weights, columns):
    zn, yn, na, nb = counts
    rows, depth, width = na + 2 * nb, a[0].shape[1], weights[0].shape[1]

    def kernel(*refs):
        a_refs, b_refs, c_refs = refs[:zn], refs[zn : 2 * zn], refs[2 * zn : 3 * zn]
        w_refs = refs[3 * zn : 4 * zn]
        out_ref, w_buf, sem = refs[4 * zn :]
        y, xl, z, xh = (lax.axis_index(axis) for axis in ("y", "xl", "z", "xh"))
        at_b = pl.multiple_of(xh * nb, nb)
        at_c = pl.multiple_of((1 - xh) * nb, nb)

        def copy(index, slot):
            return pltpu.make_async_copy(
                w_refs[index].at[:, pl.ds(columns[index], width)], w_buf.at[slot], sem.at[slot]
            )

        def start(d, slot):
            block = lax.rem(z + d, zn)
            across = lax.rem(block // 2 - y + yn, yn)
            wanted = 2 * across + jnp.where(lax.rem(block, 2) == xl, 0, 1)
            for index in range(zn):
                @pl.when(wanted == index)
                def _():
                    copy(index, slot).start()

        start(0, 0)
        for d in range(zn):
            slot = d % 2
            if d + 1 < zn:
                start(d + 1, 1 - slot)
            copy(0, slot).wait()
            for ref, first, at, n in (
                (a_refs[d], 0, 2 * nb, na),
                (b_refs[d], 0, at_b, nb),
                (c_refs[d], c_rows[d], at_c, nb),
            ):
                where = pl.ds(at, n)
                part = jnp.dot(
                    ref[first : first + n, :], w_buf[slot], preferred_element_type=jnp.float32
                )
                out_ref[where, :] = part if d == 0 else out_ref[where, :] + part

    anywhere = pl.BlockSpec(memory_space=pl.ANY)
    vmem = pl.BlockSpec(memory_space=pltpu.VMEM)
    return pl.pallas_call(
        kernel,
        out_shape=jax.ShapeDtypeStruct((rows, width), jnp.float32),
        in_specs=[vmem] * (3 * zn) + [anywhere] * zn,
        out_specs=vmem,
        scratch_shapes=[
            pltpu.VMEM((2, depth, width), jnp.bfloat16),
            pltpu.SemaphoreType.DMA((2,)),
        ],
        compiler_params=pltpu.CompilerParams(vmem_limit_bytes=8 * 1024 * 1024),
        cost_estimate=pl.CostEstimate(
            flops=2 * rows * width * depth * zn,
            bytes_accessed=2 * zn * depth * (rows + width) + 4 * rows * width,
            transcendentals=0,
        ),
    )(*a, *b, *c, *weights)


def per_device(tokens, up_weight):
    core, xh = lax.axis_index("core"), lax.axis_index("xh")
    zn, yn = lax.axis_size("z"), lax.axis_size("y")
    rows, depth = tokens.shape
    nb = 11 * rows // 40
    na = rows - 2 * nb
    width = up_weight.shape[1] // 2

    def up(axis, a):
        return lax.ppermute(a, axis, ring(lax.axis_size(axis), 1))

    def down(axis, a):
        return lax.ppermute(a, axis, ring(lax.axis_size(axis), -1))

    def crossed(a, shift):
        pairs = [
            (2 * i + k, 2 * ((i + shift) % yn) + 1 - k) for i in range(yn) for k in range(2)
        ]
        return lax.ppermute(a, ("y", "core"), pairs)

    def quarter(parity, layer):
        return lax.dynamic_slice(
            up_weight, (parity * depth, layer * width), (depth, width)
        )

    b, c, a = {}, {}, {}
    b[0] = lax.dynamic_slice_in_dim(tokens, xh * nb, nb, 0)
    c[0] = lax.dynamic_slice_in_dim(tokens, (1 - xh) * nb, nb, 0)
    a[0] = tokens[2 * nb :]
    mine, given, far = quarter(core, xh), quarter(1 - core, xh), quarter(1 - core, 1 - xh)

    b[-1], b[1] = up("z", b[0]), down("z", b[0])
    a[-1], a[1] = up("z", a[0]), down("z", a[0])
    b[-2], b[2] = up("z", b[-1]), down("z", b[1])
    a[-2], a[2] = up("z", a[-1]), down("z", a[1])
    b[-3], b[3] = up("z", b[-2]), down("z", b[2])
    a[-3], a[3] = up("z", a[-2]), down("z", a[2])
    b[4], a[4] = down("z", b[3]), up("z", a[-3])
    for d in (1, 2, 3):
        pair = lax.ppermute(jnp.concatenate([b[-d], b[d]], 0), "xh", ring(2, 1))
        c[-d], c[d] = (pair, 0), (pair, nb)
    c[0], c[4] = (c[0], 0), (lax.ppermute(b[4], "xh", ring(2, 1)), 0)

    wa, wb, wo = {0: mine}, {}, {}
    wa[-1], wa[1] = up("y", mine), down("y", mine)
    wb[-1], wb[1] = crossed(given, 1), crossed(given, -1)
    near = lax.ppermute(mine, "xl", ring(2, 1))
    across = lax.ppermute(far, ("xl", "core", "xh"), [(i, 7 - i) for i in range(8)])
    wb[0] = lax.ppermute(given, "core", ring(2, 1))
    wo[0] = jnp.concatenate([near, across], 1)
    wo[-1], wo[1] = up("y", wo[0]), down("y", wo[0])
    wide = up("y", jnp.concatenate([wa[-1], wb[-1]], 1))
    wa[2], wb[2] = wide, wide
    wo[2] = down("y", wo[1])

    def turn(pieces, size):
        return [pieces[d if d in pieces else d - size] for d in range(size)]

    counts = (zn, yn, na, nb)
    a, b, c = (turn(t, zn) for t in (a, b, c))
    tokens_in = (a, b, [t[0] for t in c], [t[1] for t in c])
    wa, wb, wo = (turn(w, yn) for w in (wa, wb, wo))

    def mixed(first):
        return [w for pair in zip(first, wo) for w in pair]

    at = [width if w is wide or i % 2 else 0 for i, w in enumerate(mixed(wb))]
    partner = block_product(counts, *tokens_in, mixed(wb), at)
    swapped = lax.ppermute(partner, "core", ring(2, 1))
    own = block_product(counts, *tokens_in, mixed(wa), (0, 0) * yn)
    return (own + swapped).astype(jnp.bfloat16)


def solution(mesh):
    split = Mesh(
        mesh.devices.reshape(4, 2, mesh.shape["col"] // 2, 2, mesh.shape["layer"]), AXES
    )
    spec = P(("y", "xl"), ("z", "core"))
    return jax.shard_map(
        per_device,
        mesh=split,
        in_specs=(spec, spec),
        out_specs=P(("y", "xl"), ("z", "core", "xh")),
        check_vma=False,
    )
```

profile of v0, /device:TPU:1, one launch (start us, length us, event | category | flops | bytes accessed | tf_op | source)
XLA Modules:
  0.0 153.3 jit_solution(335146619116667305)
XLA Ops:
  0.0 1.1 constant_dynamic-slice_fusion
  1.1 2.5 %collective-permute-start.11 = (bf16[352,512]{1,0:T(8,128)(2,1)S(1)}, bf16[352,512]{1,0:T(8,128)(2,1)S(1)}, u32[]{:S(2)}, u32[]{:S(2)}) collective-permute-start(bf16[352,512]{1,0:T(8,128)(2,1)S(1)} %get-tuple-element.9.refs_8_), channel_id=1, source_target_pairs={{0,4},{4,8},{8,12},{12,16},{16,20},{20,24},{24,28},{28,0},{1,5},{5... | collective-permute-start | bytes 1081352 | tf_op jit(solution)/shard_map/ppermute | solution.py:89
  3.7 1.5 fusion
  5.1 3.4 %collective-permute-start.19 = (bf16[512,512]{1,0:T(8,128)(2,1)S(1)}, bf16[512,512]{1,0:T(8,128)(2,1)S(1)}, u32[]{:S(2)}, u32[]{:S(2)}) collective-permute-start(bf16[512,512]{1,0:T(8,128)(2,1)S(1)} %get-tuple-element.7), channel_id=1, source_target_pairs={{0,35},{1,34},{2,33},{3,32},{32,3},{33,2},{34,1},{35,0},{4,39},{5,... | collective-permute-start | bytes 1572872 | tf_op jit(solution)/shard_map/ppermute | solution.py:127
  8.5 3.7 %collective-permute-start.7 = (bf16[352,512]{1,0:T(8,128)(2,1)S(1)}, bf16[352,512]{1,0:T(8,128)(2,1)S(1)}, u32[]{:S(2)}, u32[]{:S(2)}) collective-permute-start(bf16[352,512]{1,0:T(8,128)(2,1)S(1)} %get-tuple-element.9.refs_8_), channel_id=1, source_target_pairs={{0,28},{4,0},{8,4},{12,8},{16,12},{20,16},{24,20},{28,24},{1,29},{... | collective-permute-start | bytes 1081352 | tf_op jit(solution)/shard_map/ppermute | solution.py:92
  12.2 2.8 %collective-permute-start.28 = (bf16[512,512]{1,0:T(8,128)(2,1)S(1)}, bf16[512,512]{1,0:T(8,128)(2,1)S(1)}, u32[]{:S(2)}, u32[]{:S(2)}) collective-permute-start(bf16[512,512]{1,0:T(8,128)(2,1)S(1)} %get-tuple-element.5), channel_id=1, source_target_pairs={{0,194},{2,192},{64,2},{66,0},{128,66},{130,64},{192,130},{194,128... | collective-permute-start | bytes 1572872 | tf_op jit(solution)/shard_map/ppermute | solution.py:98
  15.0 0.4 collective-permute-start.27
  15.4 0.4 collective-permute-done.11.refs_15_
  15.7 2.4 %collective-permute-start.23 = (bf16[512,512]{1,0:T(8,128)(2,1)S(1)}, bf16[512,512]{1,0:T(8,128)(2,1)S(1)}, u32[]{:S(2)}, u32[]{:S(2)}) collective-permute-start(bf16[512,512]{1,0:T(8,128)(2,1)S(1)} %get-tuple-element.5), channel_id=1, source_target_pairs={{0,66},{2,64},{64,130},{66,128},{128,194},{130,192},{192,2},{194,0... | collective-permute-start | bytes 1572872 | tf_op jit(solution)/shard_map/ppermute | solution.py:98
  18.2 2.0 %collective-permute-done.7.refs_9_ = bf16[352,512]{1,0:T(8,128)(2,1)S(1)} collective-permute-done((bf16[352,512]{1,0:T(8,128)(2,1)S(1)}, bf16[352,512]{1,0:T(8,128)(2,1)S(1)}, u32[]{:S(2)}, u32[]{:S(2)}) %collective-permute-start.7) | collective-permute-done | bytes 360480 | tf_op jit(solution)/shard_map/ppermute | solution.py:92
  20.2 1.3 collective-permute-start.22
  21.4 0.0 collective-permute-done.19
  21.5 4.7 %collective-permute-done.28.refs_26_ = bf16[512,512]{1,0:T(8,128)(2,1)S(1)} collective-permute-done((bf16[512,512]{1,0:T(8,128)(2,1)S(1)}, bf16[512,512]{1,0:T(8,128)(2,1)S(1)}, u32[]{:S(2)}, u32[]{:S(2)}) %collective-permute-start.28) | collective-permute-done | bytes 524320 | tf_op jit(solution)/shard_map/ppermute | solution.py:98
  26.2 1.1 slice.3.refs_0_
  27.3 0.1 collective-permute-start.3
  27.4 5.0 %collective-permute-done.23.refs_30_ = bf16[512,512]{1,0:T(8,128)(2,1)S(1)} collective-permute-done((bf16[512,512]{1,0:T(8,128)(2,1)S(1)}, bf16[512,512]{1,0:T(8,128)(2,1)S(1)}, u32[]{:S(2)}, u32[]{:S(2)}) %collective-permute-start.23) | collective-permute-done | bytes 524320 | tf_op jit(solution)/shard_map/ppermute | solution.py:98
  32.4 1.2 collective-permute-start
  33.5 9.4 %collective-permute-done.22.refs_30_ = bf16[512,512]{1,0:T(8,128)(2,1)S(1)} collective-permute-done((bf16[512,512]{1,0:T(8,128)(2,1)S(1)}, bf16[512,512]{1,0:T(8,128)(2,1)S(1)}, u32[]{:S(2)}, u32[]{:S(2)}) %collective-permute-start.22) | collective-permute-done | bytes 524320 | tf_op jit(solution)/shard_map/ppermute | solution.py:89
  42.9 1.5 collective-permute-start.8
  44.4 0.0 collective-permute-start.13
  44.4 2.8 %collective-permute-start.14 = (bf16[704,512]{1,0:T(8,128)(2,1)S(1)}, bf16[704,512]{1,0:T(8,128)(2,1)S(1)}, u32[]{:S(2)}, u32[]{:S(2)}) collective-permute-start(bf16[704,512]{1,0:T(8,128)(2,1)S(1)} %pad_maximum_fusion.1), channel_id=1, source_target_pairs={{0,1},{1,0},{2,3},{3,2},{4,5},{5,4},{6,7},{7,6},{8,9},{9,8},{10,11... | collective-permute-start | bytes 2162696 | tf_op jit(solution)/shard_map/ppermute | solution.py:119
  47.3 0.1 constant_dynamic-update-slice_fusion.1
  47.3 0.1 constant_dynamic-update-slice_fusion.refs_25_
  47.4 1.7 %collective-permute-done.3.refs_7_ = bf16[576,512]{1,0:T(8,128)(2,1)S(1)} collective-permute-done((bf16[576,512]{1,0:T(8,128)(2,1)S(1)}, bf16[576,512]{1,0:T(8,128)(2,1)S(1)}, u32[]{:S(2)}, u32[]{:S(2)}) %collective-permute-start.3) | collective-permute-done | bytes 589856 | tf_op jit(solution)/shard_map/ppermute | solution.py:89
  49.1 4.4 %collective-permute-start.21 = (bf16[512,1024]{1,0:T(8,128)(2,1)S(1)}, bf16[512,1024]{1,0:T(8,128)(2,1)S(1)}, u32[]{:S(2)}, u32[]{:S(2)}) collective-permute-start(bf16[512,1024]{1,0:T(8,128)(2,1)S(1)} %constant_dynamic-update-slice_fusion.refs_25_), channel_id=1, source_target_pairs={{0,192},{64,0},{128,64},{192,128},{1,193},{65,1},{129,65},{193,129... | collective-permute-start | bytes 3145736 | tf_op jit(solution)/shard_map/ppermute | solution.py:92
  53.5 1.8 %collective-permute-done.8.refs_10_ = bf16[352,512]{1,0:T(8,128)(2,1)S(1)} collective-permute-done((bf16[352,512]{1,0:T(8,128)(2,1)S(1)}, bf16[352,512]{1,0:T(8,128)(2,1)S(1)}, u32[]{:S(2)}, u32[]{:S(2)}) %collective-permute-start.8) | collective-permute-done | bytes 360480 | tf_op jit(solution)/shard_map/ppermute | solution.py:92
  55.3 2.1 %collective-permute-start.9 = (bf16[352,512]{1,0:T(8,128)(2,1)S(1)}, bf16[352,512]{1,0:T(8,128)(2,1)S(1)}, u32[]{:S(2)}, u32[]{:S(2)}) collective-permute-start(bf16[352,512]{1,0:T(8,128)(2,1)S(1)} %collective-permute-done.8.refs_10_), channel_id=1, source_target_pairs={{0,28},{4,0},{8,4},{12,8},{16,12},{20,16},{24,20},{28,24},{1,29},{... | collective-permute-start | bytes 1081352 | tf_op jit(solution)/shard_map/ppermute | solution.py:92
  57.4 0.0 collective-permute-start.1
  57.4 0.1 pad_maximum_fusion
  57.5 7.2 %collective-permute-done.9.refs_11_ = bf16[352,512]{1,0:T(8,128)(2,1)S(1)} collective-permute-done((bf16[352,512]{1,0:T(8,128)(2,1)S(1)}, bf16[352,512]{1,0:T(8,128)(2,1)S(1)}, u32[]{:S(2)}, u32[]{:S(2)}) %collective-permute-start.9) | collective-permute-done | bytes 360480 | tf_op jit(solution)/shard_map/ppermute | solution.py:92
  64.7 2.8 %collective-permute-start.10 = (bf16[352,512]{1,0:T(8,128)(2,1)S(1)}, bf16[352,512]{1,0:T(8,128)(2,1)S(1)}, u32[]{:S(2)}, u32[]{:S(2)}) collective-permute-start(bf16[352,512]{1,0:T(8,128)(2,1)S(1)} %collective-permute-done.9.refs_11_), channel_id=1, source_target_pairs={{0,28},{4,0},{8,4},{12,8},{16,12},{20,16},{24,20},{28,24},{1,29},{... | collective-permute-start | bytes 1081352 | tf_op jit(solution)/shard_map/ppermute | solution.py:92
  67.6 1.6 %collective-permute-done.4.refs_6_ = bf16[576,512]{1,0:T(8,128)(2,1)S(1)} collective-permute-done((bf16[576,512]{1,0:T(8,128)(2,1)S(1)}, bf16[576,512]{1,0:T(8,128)(2,1)S(1)}, u32[]{:S(2)}, u32[]{:S(2)}) %collective-permute-start.4) | collective-permute-done | bytes 589856 | tf_op jit(solution)/shard_map/ppermute | solution.py:89
  69.3 1.4 collective-permute-start.15
  70.6 6.7 %collective-permute-done.1.refs_2_ = bf16[576,512]{1,0:T(8,128)(2,1)S(1)} collective-permute-done((bf16[576,512]{1,0:T(8,128)(2,1)S(1)}, bf16[576,512]{1,0:T(8,128)(2,1)S(1)}, u32[]{:S(2)}, u32[]{:S(2)}) %collective-permute-start.1) | collective-permute-done | bytes 589856 | tf_op jit(solution)/shard_map/ppermute | solution.py:92
  77.4 7.7 %collective-permute-done.10.refs_12_ = bf16[352,512]{1,0:T(8,128)(2,1)S(1)} collective-permute-done((bf16[352,512]{1,0:T(8,128)(2,1)S(1)}, bf16[352,512]{1,0:T(8,128)(2,1)S(1)}, u32[]{:S(2)}, u32[]{:S(2)}) %collective-permute-start.10) | collective-permute-done | bytes 360480 | tf_op jit(solution)/shard_map/ppermute | solution.py:92
  85.1 1.1 collective-permute-start.25
  86.3 0.1 collective-permute-done.15.refs_18_.refs_22_
  86.4 1.6 %collective-permute-start.16 = (bf16[704,512]{1,0:T(8,128)(2,1)S(1)}, bf16[704,512]{1,0:T(8,128)(2,1)S(1)}, u32[]{:S(2)}, u32[]{:S(2)}) collective-permute-start(bf16[704,512]{1,0:T(8,128)(2,1)S(1)} %pad_maximum_fusion.3), channel_id=1, source_target_pairs={{0,1},{1,0},{2,3},{3,2},{4,5},{5,4},{6,7},{7,6},{8,9},{9,8},{10,11... | collective-permute-start | bytes 2162696 | tf_op jit(solution)/shard_map/ppermute | solution.py:119
  88.0 3.0 %collective-permute-start.2 = (bf16[576,512]{1,0:T(8,128)(2,1)S(1)}, bf16[576,512]{1,0:T(8,128)(2,1)S(1)}, u32[]{:S(2)}, u32[]{:S(2)}) collective-permute-start(bf16[576,512]{1,0:T(8,128)(2,1)S(1)} %collective-permute-done.1.refs_2_), channel_id=1, source_target_pairs={{0,28},{4,0},{8,4},{12,8},{16,12},{20,16},{24,20},{28,24},{1,29},{... | collective-permute-start | bytes 1769480 | tf_op jit(solution)/shard_map/ppermute | solution.py:92
  91.0 8.8 %collective-permute-done.5.refs_5_ = bf16[576,512]{1,0:T(8,128)(2,1)S(1)} collective-permute-done((bf16[576,512]{1,0:T(8,128)(2,1)S(1)}, bf16[576,512]{1,0:T(8,128)(2,1)S(1)}, u32[]{:S(2)}, u32[]{:S(2)}) %collective-permute-start.5) | collective-permute-done | bytes 589856 | tf_op jit(solution)/shard_map/ppermute | solution.py:89
  99.8 10.6 %collective-permute-done.26.refs_31_ = bf16[512,1024]{1,0:T(8,128)(2,1)S(1)} collective-permute-done((bf16[512,1024]{1,0:T(8,128)(2,1)S(1)}, bf16[512,1024]{1,0:T(8,128)(2,1)S(1)}, u32[]{:S(2)}, u32[]{:S(2)}) %collective-permute-start.26) | collective-permute-done | bytes 1048608 | tf_op jit(solution)/shard_map/ppermute | solution.py:89
  110.4 2.9 %collective-permute-start.17 = (bf16[352,512]{1,0:T(8,128)(2,1)S(1)}, bf16[352,512]{1,0:T(8,128)(2,1)S(1)}, u32[]{:S(2)}, u32[]{:S(2)}) collective-permute-start(bf16[352,512]{1,0:T(8,128)(2,1)S(1)} %collective-permute-done.10.refs_12_), channel_id=1, source_target_pairs={{0,1},{1,0},{2,3},{3,2},{4,5},{5,4},{6,7},{7,6},{8,9},{9,8},{10,11... | collective-permute-start | bytes 1081352 | tf_op jit(solution)/shard_map/ppermute | solution.py:121
  113.3 4.9 %collective-permute-done.17.refs_20_ = bf16[352,512]{1,0:T(8,128)(2,1)S(1)} collective-permute-done((bf16[352,512]{1,0:T(8,128)(2,1)S(1)}, bf16[352,512]{1,0:T(8,128)(2,1)S(1)}, u32[]{:S(2)}, u32[]{:S(2)}) %collective-permute-start.17) | collective-permute-done | bytes 360480 | tf_op jit(solution)/shard_map/ppermute | solution.py:121
  118.2 7.8 %shard_map.29 = f32[1280,512]{1,0:T(8,128)S(1)} custom-call(bf16[576,512]{1,0:T(8,128)(2,1)S(1)} %slice.3.refs_0_, bf16[576,512]{1,0:T(8,128)(2,1)S(1)} %collective-permute-done.refs_1_, bf16[576,512]{1,0:T(8,128)(2,1)S(1)} %collective-permute-done.1.refs_2_, bf16[576,512]{1,0:T(8,128)(2,1)S(1)} %collective-permute-done.2.refs_3_, ...), custom_call_target="tpu_custom_call" | custom-call | flops 5368709120 | bytes 17301504 | tf_op jit(solution)/shard_map/pallas_call | solution.py:62
  126.0 4.8 %collective-permute-start.29 = (f32[1280,512]{1,0:T(8,128)S(1)}, f32[1280,512]{1,0:T(8,128)S(1)}, u32[]{:S(2)}, u32[]{:S(2)}) collective-permute-start(f32[1280,512]{1,0:T(8,128)S(1)} %shard_map.29), channel_id=1, source_target_pairs={{0,2},{2,0},{1,3},{3,1},{4,6},{6,4},{5,7},{7,5},{8,10},{10,8},{9,1... | collective-permute-start | bytes 7864328 | tf_op jit(solution)/shard_map/ppermute | solution.py:148
  130.8 13.4 %collective-permute-done.20.refs_26_ = bf16[512,512]{1,0:T(8,128)(2,1)S(1)} collective-permute-done((bf16[512,512]{1,0:T(8,128)(2,1)S(1)}, bf16[512,512]{1,0:T(8,128)(2,1)S(1)}, u32[]{:S(2)}, u32[]{:S(2)}) %collective-permute-start.20) | collective-permute-done | bytes 524320 | tf_op jit(solution)/shard_map/ppermute | solution.py:92
  144.2 7.5 %shard_map.28 = f32[1280,512]{1,0:T(8,128)S(1)} custom-call(bf16[576,512]{1,0:T(8,128)(2,1)S(1)} %slice.3.refs_0_, bf16[576,512]{1,0:T(8,128)(2,1)S(1)} %collective-permute-done.refs_1_, bf16[576,512]{1,0:T(8,128)(2,1)S(1)} %collective-permute-done.1.refs_2_, bf16[576,512]{1,0:T(8,128)(2,1)S(1)} %collective-permute-done.2.refs_3_, ...), custom_call_target="tpu_custom_call" | custom-call | flops 5368709120 | bytes 17301504 | tf_op jit(solution)/shard_map/pallas_call | solution.py:62
  151.8 1.5 add_convert_fusion
  (24 shorter events, 0.2 us)
Async XLA Ops:
  1.1 14.6 %collective-permute-start.11 = (bf16[352,512]{1,0:T(8,128)(2,1)S(1)}, bf16[352,512]{1,0:T(8,128)(2,1)S(1)}, u32[]{:S(2)}, u32[]{:S(2)}) collective-permute-start(bf16[352,512]{1,0:T(8,128)(2,1)S(1)} %get-tuple-element.9.refs_8_), channel_id=1, source_target_pairs={{0,4},{4,8},{8,12},{12,16},{16,20},{20,24},{24,28},{28,0},{1,5},{5... | collective-permute-start | bytes 1081352 | tf_op jit(solution)/shard_map/ppermute | solution.py:89
  5.1 16.3 %collective-permute-start.19 = (bf16[512,512]{1,0:T(8,128)(2,1)S(1)}, bf16[512,512]{1,0:T(8,128)(2,1)S(1)}, u32[]{:S(2)}, u32[]{:S(2)}) collective-permute-start(bf16[512,512]{1,0:T(8,128)(2,1)S(1)} %get-tuple-element.7), channel_id=1, source_target_pairs={{0,35},{1,34},{2,33},{3,32},{32,3},{33,2},{34,1},{35,0},{4,39},{5,... | collective-permute-start | bytes 1572872 | tf_op jit(solution)/shard_map/ppermute | solution.py:127
  8.5 11.6 %collective-permute-start.7 = (bf16[352,512]{1,0:T(8,128)(2,1)S(1)}, bf16[352,512]{1,0:T(8,128)(2,1)S(1)}, u32[]{:S(2)}, u32[]{:S(2)}) collective-permute-start(bf16[352,512]{1,0:T(8,128)(2,1)S(1)} %get-tuple-element.9.refs_8_), channel_id=1, source_target_pairs={{0,28},{4,0},{8,4},{12,8},{16,12},{20,16},{24,20},{28,24},{1,29},{... | collective-permute-start | bytes 1081352 | tf_op jit(solution)/shard_map/ppermute | solution.py:92
  12.2 14.0 %collective-permute-start.28 = (bf16[512,512]{1,0:T(8,128)(2,1)S(1)}, bf16[512,512]{1,0:T(8,128)(2,1)S(1)}, u32[]{:S(2)}, u32[]{:S(2)}) collective-permute-start(bf16[512,512]{1,0:T(8,128)(2,1)S(1)} %get-tuple-element.5), channel_id=1, source_target_pairs={{0,194},{2,192},{64,2},{66,0},{128,66},{130,64},{192,130},{194,128... | collective-permute-start | bytes 1572872 | tf_op jit(solution)/shard_map/ppermute | solution.py:98
  15.0 12.3 %collective-permute-start.27 = (bf16[512,512]{1,0:T(8,128)(2,1)S(1)}, bf16[512,512]{1,0:T(8,128)(2,1)S(1)}, u32[]{:S(2)}, u32[]{:S(2)}) collective-permute-start(bf16[512,512]{1,0:T(8,128)(2,1)S(1)} %get-tuple-element.5), channel_id=1, source_target_pairs={{0,2},{2,0},{1,3},{3,1},{4,6},{6,4},{5,7},{7,5},{8,10},{10,8},{9,1... | collective-permute-start | bytes 1572872 | tf_op jit(solution)/shard_map/ppermute | solution.py:128
  15.7 16.6 %collective-permute-start.23 = (bf16[512,512]{1,0:T(8,128)(2,1)S(1)}, bf16[512,512]{1,0:T(8,128)(2,1)S(1)}, u32[]{:S(2)}, u32[]{:S(2)}) collective-permute-start(bf16[512,512]{1,0:T(8,128)(2,1)S(1)} %get-tuple-element.5), channel_id=1, source_target_pairs={{0,66},{2,64},{64,130},{66,128},{128,194},{130,192},{192,2},{194,0... | collective-permute-start | bytes 1572872 | tf_op jit(solution)/shard_map/ppermute | solution.py:98
  20.2 22.7 %collective-permute-start.22 = (bf16[512,512]{1,0:T(8,128)(2,1)S(1)}, bf16[512,512]{1,0:T(8,128)(2,1)S(1)}, u32[]{:S(2)}, u32[]{:S(2)}) collective-permute-start(bf16[512,512]{1,0:T(8,128)(2,1)S(1)} %get-tuple-element.6.refs_24_), channel_id=1, source_target_pairs={{0,64},{64,128},{128,192},{192,0},{1,65},{65,129},{129,193},{193,1... | collective-permute-start | bytes 1572872 | tf_op jit(solution)/shard_map/ppermute | solution.py:89
  21.5 23.0 %collective-permute-start.18 = (bf16[512,512]{1,0:T(8,128)(2,1)S(1)}, bf16[512,512]{1,0:T(8,128)(2,1)S(1)}, u32[]{:S(2)}, u32[]{:S(2)}) collective-permute-start(bf16[512,512]{1,0:T(8,128)(2,1)S(1)} %get-tuple-element.6.refs_24_), channel_id=1, source_target_pairs={{0,32},{32,0},{1,33},{33,1},{2,34},{34,2},{3,35},{35,3},{4,36},{36... | collective-permute-start | bytes 1572872 | tf_op jit(solution)/shard_map/ppermute | solution.py:126
  26.2 18.2 %collective-permute-start.12 = (bf16[352,512]{1,0:T(8,128)(2,1)S(1)}, bf16[352,512]{1,0:T(8,128)(2,1)S(1)}, u32[]{:S(2)}, u32[]{:S(2)}) collective-permute-start(bf16[352,512]{1,0:T(8,128)(2,1)S(1)} %collective-permute-done.11.refs_15_), channel_id=1, source_target_pairs={{0,4},{4,8},{8,12},{12,16},{16,20},{20,24},{24,28},{28,0},{1,5},{5... | collective-permute-start | bytes 1081352 | tf_op jit(solution)/shard_map/ppermute | solution.py:89
  27.3 21.8 %collective-permute-start.3 = (bf16[576,512]{1,0:T(8,128)(2,1)S(1)}, bf16[576,512]{1,0:T(8,128)(2,1)S(1)}, u32[]{:S(2)}, u32[]{:S(2)}) collective-permute-start(bf16[576,512]{1,0:T(8,128)(2,1)S(1)} %slice.3.refs_0_), channel_id=1, source_target_pairs={{0,4},{4,8},{8,12},{12,16},{16,20},{20,24},{24,28},{28,0},{1,5},{5... | collective-permute-start | bytes 1769480 | tf_op jit(solution)/shard_map/ppermute | solution.py:89
  32.4 21.2 %collective-permute-start = (bf16[576,512]{1,0:T(8,128)(2,1)S(1)}, bf16[576,512]{1,0:T(8,128)(2,1)S(1)}, u32[]{:S(2)}, u32[]{:S(2)}) collective-permute-start(bf16[576,512]{1,0:T(8,128)(2,1)S(1)} %slice.3.refs_0_), channel_id=1, source_target_pairs={{0,28},{4,0},{8,4},{12,8},{16,12},{20,16},{24,20},{28,24},{1,29},{... | collective-permute-start | bytes 1769480 | tf_op jit(solution)/shard_map/ppermute | solution.py:92
  42.9 12.4 %collective-permute-start.8 = (bf16[352,512]{1,0:T(8,128)(2,1)S(1)}, bf16[352,512]{1,0:T(8,128)(2,1)S(1)}, u32[]{:S(2)}, u32[]{:S(2)}) collective-permute-start(bf16[352,512]{1,0:T(8,128)(2,1)S(1)} %collective-permute-done.7.refs_9_), channel_id=1, source_target_pairs={{0,28},{4,0},{8,4},{12,8},{16,12},{20,16},{24,20},{28,24},{1,29},{... | collective-permute-start | bytes 1081352 | tf_op jit(solution)/shard_map/ppermute | solution.py:92
  44.4 13.0 %collective-permute-start.13 = (bf16[352,512]{1,0:T(8,128)(2,1)S(1)}, bf16[352,512]{1,0:T(8,128)(2,1)S(1)}, u32[]{:S(2)}, u32[]{:S(2)}) collective-permute-start(bf16[352,512]{1,0:T(8,128)(2,1)S(1)} %collective-permute-done.12.refs_14_), channel_id=1, source_target_pairs={{0,4},{4,8},{8,12},{12,16},{16,20},{20,24},{24,28},{28,0},{1,5},{5... | collective-permute-start | bytes 1081352 | tf_op jit(solution)/shard_map/ppermute | solution.py:89
  44.4 20.3 %collective-permute-start.14 = (bf16[704,512]{1,0:T(8,128)(2,1)S(1)}, bf16[704,512]{1,0:T(8,128)(2,1)S(1)}, u32[]{:S(2)}, u32[]{:S(2)}) collective-permute-start(bf16[704,512]{1,0:T(8,128)(2,1)S(1)} %pad_maximum_fusion.1), channel_id=1, source_target_pairs={{0,1},{1,0},{2,3},{3,2},{4,5},{5,4},{6,7},{7,6},{8,9},{9,8},{10,11... | collective-permute-start | bytes 2162696 | tf_op jit(solution)/shard_map/ppermute | solution.py:119
  49.1 36.0 %collective-permute-start.21 = (bf16[512,1024]{1,0:T(8,128)(2,1)S(1)}, bf16[512,1024]{1,0:T(8,128)(2,1)S(1)}, u32[]{:S(2)}, u32[]{:S(2)}) collective-permute-start(bf16[512,1024]{1,0:T(8,128)(2,1)S(1)} %constant_dynamic-update-slice_fusion.refs_25_), channel_id=1, source_target_pairs={{0,192},{64,0},{128,64},{192,128},{1,193},{65,1},{129,65},{193,129... | collective-permute-start | bytes 3145736 | tf_op jit(solution)/shard_map/ppermute | solution.py:92
  53.5 15.7 %collective-permute-start.4 = (bf16[576,512]{1,0:T(8,128)(2,1)S(1)}, bf16[576,512]{1,0:T(8,128)(2,1)S(1)}, u32[]{:S(2)}, u32[]{:S(2)}) collective-permute-start(bf16[576,512]{1,0:T(8,128)(2,1)S(1)} %collective-permute-done.3.refs_7_), channel_id=1, source_target_pairs={{0,4},{4,8},{8,12},{12,16},{16,20},{20,24},{24,28},{28,0},{1,5},{5... | collective-permute-start | bytes 1769480 | tf_op jit(solution)/shard_map/ppermute | solution.py:89
  55.3 9.4 %collective-permute-start.9 = (bf16[352,512]{1,0:T(8,128)(2,1)S(1)}, bf16[352,512]{1,0:T(8,128)(2,1)S(1)}, u32[]{:S(2)}, u32[]{:S(2)}) collective-permute-start(bf16[352,512]{1,0:T(8,128)(2,1)S(1)} %collective-permute-done.8.refs_10_), channel_id=1, source_target_pairs={{0,28},{4,0},{8,4},{12,8},{16,12},{20,16},{24,20},{28,24},{1,29},{... | collective-permute-start | bytes 1081352 | tf_op jit(solution)/shard_map/ppermute | solution.py:92
  57.4 20.0 %collective-permute-start.1 = (bf16[576,512]{1,0:T(8,128)(2,1)S(1)}, bf16[576,512]{1,0:T(8,128)(2,1)S(1)}, u32[]{:S(2)}, u32[]{:S(2)}) collective-permute-start(bf16[576,512]{1,0:T(8,128)(2,1)S(1)} %collective-permute-done.refs_1_), channel_id=1, source_target_pairs={{0,28},{4,0},{8,4},{12,8},{16,12},{20,16},{24,20},{28,24},{1,29},{... | collective-permute-start | bytes 1769480 | tf_op jit(solution)/shard_map/ppermute | solution.py:92
  64.7 23.3 %collective-permute-start.24 = (bf16[512,1024]{1,0:T(8,128)(2,1)S(1)}, bf16[512,1024]{1,0:T(8,128)(2,1)S(1)}, u32[]{:S(2)}, u32[]{:S(2)}) collective-permute-start(bf16[512,1024]{1,0:T(8,128)(2,1)S(1)} %pad_maximum_fusion), channel_id=1, source_target_pairs={{0,64},{64,128},{128,192},{192,0},{1,65},{65,129},{129,193},{193,1... | collective-permute-start | bytes 3145736 | tf_op jit(solution)/shard_map/ppermute | solution.py:89
  64.7 20.4 %collective-permute-start.10 = (bf16[352,512]{1,0:T(8,128)(2,1)S(1)}, bf16[352,512]{1,0:T(8,128)(2,1)S(1)}, u32[]{:S(2)}, u32[]{:S(2)}) collective-permute-start(bf16[352,512]{1,0:T(8,128)(2,1)S(1)} %collective-permute-done.9.refs_11_), channel_id=1, source_target_pairs={{0,28},{4,0},{8,4},{12,8},{16,12},{20,16},{24,20},{28,24},{1,29},{... | collective-permute-start | bytes 1081352 | tf_op jit(solution)/shard_map/ppermute | solution.py:92
  69.3 17.2 %collective-permute-start.15 = (bf16[704,512]{1,0:T(8,128)(2,1)S(1)}, bf16[704,512]{1,0:T(8,128)(2,1)S(1)}, u32[]{:S(2)}, u32[]{:S(2)}) collective-permute-start(bf16[704,512]{1,0:T(8,128)(2,1)S(1)} %pad_maximum_fusion.2), channel_id=1, source_target_pairs={{0,1},{1,0},{2,3},{3,2},{4,5},{5,4},{6,7},{7,6},{8,9},{9,8},{10,11... | collective-permute-start | bytes 2162696 | tf_op jit(solution)/shard_map/ppermute | solution.py:119
  77.4 33.0 %collective-permute-start.26 = (bf16[512,1024]{1,0:T(8,128)(2,1)S(1)}, bf16[512,1024]{1,0:T(8,128)(2,1)S(1)}, u32[]{:S(2)}, u32[]{:S(2)}) collective-permute-start(bf16[512,1024]{1,0:T(8,128)(2,1)S(1)} %constant_dynamic-update-slice_fusion.refs_25_), channel_id=1, source_target_pairs={{0,64},{64,128},{128,192},{192,0},{1,65},{65,129},{129,193},{193,1... | collective-permute-start | bytes 3145736 | tf_op jit(solution)/shard_map/ppermute | solution.py:89
  85.1 14.7 %collective-permute-start.5 = (bf16[576,512]{1,0:T(8,128)(2,1)S(1)}, bf16[576,512]{1,0:T(8,128)(2,1)S(1)}, u32[]{:S(2)}, u32[]{:S(2)}) collective-permute-start(bf16[576,512]{1,0:T(8,128)(2,1)S(1)} %collective-permute-done.4.refs_6_), channel_id=1, source_target_pairs={{0,4},{4,8},{8,12},{12,16},{16,20},{20,24},{24,28},{28,0},{1,5},{5... | collective-permute-start | bytes 1769480 | tf_op jit(solution)/shard_map/ppermute | solution.py:89
  85.1 33.1 %collective-permute-start.25 = (bf16[512,1024]{1,0:T(8,128)(2,1)S(1)}, bf16[512,1024]{1,0:T(8,128)(2,1)S(1)}, u32[]{:S(2)}, u32[]{:S(2)}) collective-permute-start(bf16[512,1024]{1,0:T(8,128)(2,1)S(1)} %collective-permute-done.21.refs_27_), channel_id=1, source_target_pairs={{0,192},{64,0},{128,64},{192,128},{1,193},{65,1},{129,65},{193,129... | collective-permute-start | bytes 3145736 | tf_op jit(solution)/shard_map/ppermute | solution.py:92
  86.4 31.7 %collective-permute-start.16 = (bf16[704,512]{1,0:T(8,128)(2,1)S(1)}, bf16[704,512]{1,0:T(8,128)(2,1)S(1)}, u32[]{:S(2)}, u32[]{:S(2)}) collective-permute-start(bf16[704,512]{1,0:T(8,128)(2,1)S(1)} %pad_maximum_fusion.3), channel_id=1, source_target_pairs={{0,1},{1,0},{2,3},{3,2},{4,5},{5,4},{6,7},{7,6},{8,9},{9,8},{10,11... | collective-permute-start | bytes 2162696 | tf_op jit(solution)/shard_map/ppermute | solution.py:119
  88.0 25.3 %collective-permute-start.2 = (bf16[576,512]{1,0:T(8,128)(2,1)S(1)}, bf16[576,512]{1,0:T(8,128)(2,1)S(1)}, u32[]{:S(2)}, u32[]{:S(2)}) collective-permute-start(bf16[576,512]{1,0:T(8,128)(2,1)S(1)} %collective-permute-done.1.refs_2_), channel_id=1, source_target_pairs={{0,28},{4,0},{8,4},{12,8},{16,12},{20,16},{24,20},{28,24},{1,29},{... | collective-permute-start | bytes 1769480 | tf_op jit(solution)/shard_map/ppermute | solution.py:92
  99.8 18.4 %collective-permute-start.6 = (bf16[576,512]{1,0:T(8,128)(2,1)S(1)}, bf16[576,512]{1,0:T(8,128)(2,1)S(1)}, u32[]{:S(2)}, u32[]{:S(2)}) collective-permute-start(bf16[576,512]{1,0:T(8,128)(2,1)S(1)} %collective-permute-done.5.refs_5_), channel_id=1, source_target_pairs={{0,4},{4,8},{8,12},{12,16},{16,20},{20,24},{24,28},{28,0},{1,5},{5... | collective-permute-start | bytes 1769480 | tf_op jit(solution)/shard_map/ppermute | solution.py:89
  110.4 7.8 %collective-permute-start.17 = (bf16[352,512]{1,0:T(8,128)(2,1)S(1)}, bf16[352,512]{1,0:T(8,128)(2,1)S(1)}, u32[]{:S(2)}, u32[]{:S(2)}) collective-permute-start(bf16[352,512]{1,0:T(8,128)(2,1)S(1)} %collective-permute-done.10.refs_12_), channel_id=1, source_target_pairs={{0,1},{1,0},{2,3},{3,2},{4,5},{5,4},{6,7},{7,6},{8,9},{9,8},{10,11... | collective-permute-start | bytes 1081352 | tf_op jit(solution)/shard_map/ppermute | solution.py:121
  126.0 25.7 %collective-permute-start.29 = (f32[1280,512]{1,0:T(8,128)S(1)}, f32[1280,512]{1,0:T(8,128)S(1)}, u32[]{:S(2)}, u32[]{:S(2)}) collective-permute-start(f32[1280,512]{1,0:T(8,128)S(1)} %shard_map.29), channel_id=1, source_target_pairs={{0,2},{2,0},{1,3},{3,1},{4,6},{6,4},{5,7},{7,5},{8,10},{10,8},{9,1... | collective-permute-start | bytes 7864328 | tf_op jit(solution)/shard_map/ppermute | solution.py:148
  130.8 13.4 %collective-permute-start.20 = (bf16[512,512]{1,0:T(8,128)(2,1)S(1)}, bf16[512,512]{1,0:T(8,128)(2,1)S(1)}, u32[]{:S(2)}, u32[]{:S(2)}) collective-permute-start(bf16[512,512]{1,0:T(8,128)(2,1)S(1)} %get-tuple-element.6.refs_24_), channel_id=1, source_target_pairs={{0,192},{64,0},{128,64},{192,128},{1,193},{65,1},{129,65},{193,129... | collective-permute-start | bytes 1572872 | tf_op jit(solution)/shard_map/ppermute | solution.py:92
where the time goes:
time: 154 us; the launch traced here: 153 us
  waiting for transfers between devices  86 us (56%)
  starting transfers between devices  46.2 us (30%)
  Pallas kernels  15.3 us (10%)
  local copies, waits for them, and re-layouts  3.84 us (2%)
  other arithmetic  1.78 us (1%)
    ppermute x10, waiting for transfers between devices, down(): return lax.ppermute(a, axis, ring(lax.axis_size(axis), -1))  38.8 us
    ppermute x10, waiting for transfers between devices, up(): return lax.ppermute(a, axis, ring(lax.axis_size(axis), 1))  32.5 us
    ppermute x10, starting transfers between devices, down(): return lax.ppermute(a, axis, ring(lax.axis_size(axis), -1))  19.8 us
    pallas_call x2, Pallas kernels, block_product(): pl.pallas_call(kernel, out_shape=jax.ShapeDtypeStruct((rows, width), jnp....  15.3 us
    ppermute x2, waiting for transfers between devices, crossed(): return lax.ppermute(a, ('y', 'core'), pairs)  9.71 us
    ppermute x3, starting transfers between devices, per_device(): pair = lax.ppermute(jnp.concatenate([b[-d], b[d]], 0), 'xh', ring(2, 1))  5.75 us
    ppermute x2, starting transfers between devices, crossed(): return lax.ppermute(a, ('y', 'core'), pairs)  5.19 us
    ppermute x1, waiting for transfers between devices, per_device(): c[0], c[4] = ((c[0], 0), (lax.ppermute(b[4], 'xh', ring(2, 1)), 0))  4.88 us
  transfers between devices with their start and end apart: 30, of which 16 were waited for; matrix products, arithmetic and copies ran while one was open for 2% of the time, Pallas kernels for 5%

commit v1 on v0

v1 whole, which is shorter than its diff:
```python
import jax
import jax.numpy as jnp
from jax import lax
from jax.experimental import pallas as pl
from jax.experimental.pallas import tpu as pltpu
from jax.sharding import Mesh
from jax.sharding import PartitionSpec as P


AXES = ("y", "xl", "z", "core", "xh")
NEAR = (0, 1, 2, -1, -2)
LATE = (3, -3, 4)


def ring(size, shift):
    return [(i, (i + shift) % size) for i in range(size)]


VMEM = pl.BlockSpec(memory_space=pltpu.VMEM)


def room(shapes):
    return pl.pallas_call(
        lambda *refs: None,
        name="room",
        out_shape=[jax.ShapeDtypeStruct(shape, jnp.bfloat16) for shape in shapes],
        out_specs=[pl.BlockSpec(memory_space=pl.ANY)] * len(shapes),
    )()


def add_product(out_ref, tokens_ref, weight):
    rows = out_ref.shape[0]
    for first in range(0, rows, rows // 2):
        at = slice(first, first + rows // 2)
        out_ref[at, :] += jnp.dot(
            tokens_ref[at, :], weight, preferred_element_type=jnp.float32
        )


def met(d, zn, yn):
    block = lax.rem(lax.axis_index("z") + d + zn, zn)
    return lax.rem(block // 2 - lax.axis_index("y") + yn, yn), lax.rem(block, 2)


def call(kernel, rows, width, depth, blocks, args, aliases):
    return pl.pallas_call(
        kernel,
        out_shape=jax.ShapeDtypeStruct((rows, width), jnp.float32),
        in_specs=[VMEM] * len(args),
        out_specs=VMEM,
        input_output_aliases=aliases,
        compiler_params=pltpu.CompilerParams(vmem_limit_bytes=4 * 1024 * 1024),
        cost_estimate=pl.CostEstimate(
            flops=2 * rows * width * depth * blocks,
            bytes_accessed=2 * blocks * depth * (rows + width) + 8 * rows * width,
            transcendentals=0,
        ),
    )(*args)


def early_product(t_near, w_near, half, zn, yn):
    rows, depth = t_near.shape[1:]
    width = w_near.shape[2] // 2
    columns = slice(half * width, (half + 1) * width)

    def kernel(t_ref, w_ref, out_ref):
        out_ref[...] = jnp.zeros_like(out_ref)

        def block(i, carry):
            d = jnp.where(i <= 2, i, 2 - i)
            across, _ = met(d, zn, yn)

            @pl.when(across != yn // 2)
            def _():
                at = lax.rem(d + zn, zn)
                add_product(out_ref, t_ref.at[i], w_ref[at, :, columns])

            return carry

        lax.fori_loop(0, len(NEAR), block, 0)

    return call(kernel, rows, width, depth, len(NEAR), (t_near, w_near), {})


def final_product(total, t_near, t_late, w_near, w_late, half, zn, yn):
    rows, depth = t_near.shape[1:]
    width = w_near.shape[2] // 2
    columns = slice(half * width, (half + 1) * width)

    def kernel(total_ref, tn_ref, tl_ref, wn_ref, wl_ref, out_ref):
        def near(i, carry):
            across, side = met(jnp.where(i <= 2, i, 2 - i), zn, yn)

            @pl.when(across == yn // 2)
            def _():
                add_product(out_ref, tn_ref.at[i], wl_ref[side, :, columns])

            return carry

        def late(i, carry):
            d = jnp.where(i == 0, 3, jnp.where(i == 1, -3, 4))
            across, side = met(d, zn, yn)

            @pl.when(across != yn // 2)
            def _():
                add_product(out_ref, tl_ref.at[i], wn_ref[lax.rem(d + zn, zn), :, columns])

            @pl.when(across == yn // 2)
            def _():
                add_product(out_ref, tl_ref.at[i], wl_ref[side, :, columns])

            return carry

        lax.fori_loop(0, len(NEAR), near, 0)
        lax.fori_loop(0, len(LATE), late, 0)

    args = (total, t_near, t_late, w_near, w_late)
    return call(kernel, rows, width, depth, len(LATE), args, {0: 0})


def per_device(tokens, up_weight):
    y, xl, z, core, xh = (lax.axis_index(axis) for axis in AXES)
    zn, yn = lax.axis_size("z"), lax.axis_size("y")
    rows, depth = tokens.shape
    nb = 11 * rows // 40
    width = up_weight.shape[1] // 2

    def up(axis, a):
        return lax.ppermute(a, axis, ring(lax.axis_size(axis), 1))

    def down(axis, a):
        return lax.ppermute(a, axis, ring(lax.axis_size(axis), -1))

    def crossed(a, shift):
        pairs = [
            (2 * i + k, 2 * ((i + shift) % yn) + 1 - k) for i in range(yn) for k in range(2)
        ]
        return lax.ppermute(a, ("y", "core"), pairs)

    def quarter(parity, layer):
        return lax.dynamic_slice(
            up_weight, (parity * depth, layer * width), (depth, width)
        )

    b, c, a = {}, {}, {}
    b[0] = lax.dynamic_slice_in_dim(tokens, xh * nb, nb, 0)
    c[0] = lax.dynamic_slice_in_dim(tokens, (1 - xh) * nb, nb, 0)
    a[0] = tokens[2 * nb :]
    mine, given, far = quarter(core, xh), quarter(1 - core, xh), quarter(1 - core, 1 - xh)

    b[-1], b[1] = up("z", b[0]), down("z", b[0])
    a[-1], a[1] = up("z", a[0]), down("z", a[0])
    b[-2], b[2] = up("z", b[-1]), down("z", b[1])
    a[-2], a[2] = up("z", a[-1]), down("z", a[1])
    b[-3], b[3] = up("z", b[-2]), down("z", b[2])
    a[-3], a[3] = up("z", a[-2]), down("z", a[2])
    b[4], a[4] = down("z", b[3]), up("z", a[-3])
    for d in (1, 2, 3):
        pair = lax.ppermute(jnp.concatenate([b[-d], b[d]], 0), "xh", ring(2, 1))
        c[-d], c[d] = (pair, 0), (pair, nb)
    c[0], c[4] = (c[0], 0), (lax.ppermute(b[4], "xh", ring(2, 1)), 0)

    wa, wb, wo = {0: mine}, {}, {}
    wa[-1], wa[1] = up("y", mine), down("y", mine)
    wb[-1], wb[1] = crossed(given, 1), crossed(given, -1)
    near = lax.ppermute(mine, "xl", ring(2, 1))
    across = lax.ppermute(far, ("xl", "core", "xh"), [(i, 7 - i) for i in range(8)])
    wb[0] = lax.ppermute(given, "core", ring(2, 1))
    wo[0] = jnp.concatenate([near, across], 1)
    wo[-1], wo[1] = up("y", wo[0]), down("y", wo[0])
    wide = up("y", jnp.concatenate([wa[-1], wb[-1]], 1))
    wo[2] = down("y", wo[1])

    t_near, t_late, w_near, w_late = room(
        (
            (len(NEAR), rows, depth),
            (len(LATE), rows, depth),
            (zn, depth, 2 * width),
            (2, depth, 2 * width),
        )
    )

    def put(stack, piece, *at):
        return lax.dynamic_update_slice(stack, piece[None], at)

    def put_tokens(stack, order):
        for i, d in enumerate(order):
            pair, first = c[d]
            stack = put(stack, a[d], i, 2 * nb, 0)
            stack = put(stack, b[d], i, xh * nb, 0)
            stack = put(stack, pair[first : first + nb], i, (1 - xh) * nb, 0)
        return stack

    t_near, t_late = put_tokens(t_near, NEAR), put_tokens(t_late, LATE)
    for dy in (0, -1, 1):
        row = 2 * lax.rem(y + dy + yn, yn) - z + 2 * zn
        own, other = lax.rem(row + xl, zn), lax.rem(row + 1 - xl, zn)
        w_near = put(w_near, wa[dy], own, 0, 0)
        w_near = put(w_near, wb[dy], own, 0, width)
        w_near = put(w_near, wo[dy], other, 0, 0)
    w_late = put(w_late, wide, xl, 0, 0)
    w_late = put(w_late, wo[2], 1 - xl, 0, 0)

    total = {}
    for half in (1, 0):
        total[half] = early_product(t_near, w_near, half, zn, yn)
    rest = (t_near, t_late, w_near, w_late)
    partner = final_product(total[1], *rest, 1, zn, yn)
    swapped = lax.ppermute(partner, "core", ring(2, 1))
    own = final_product(total[0], *rest, 0, zn, yn)
    return (own + swapped).astype(jnp.bfloat16)


def solution(mesh):
    split = Mesh(
        mesh.devices.reshape(4, 2, mesh.shape["col"] // 2, 2, mesh.shape["layer"]), AXES
    )
    spec = P(("y", "xl"), ("z", "core"))
    return jax.shard_map(
        per_device,
        mesh=split,
        in_specs=(spec, spec),
        out_specs=P(("y", "xl"), ("z", "core", "xh")),
        check_vma=False,
    )
```

time: 154 us -> 172 us (1.12)
  local copies, waits for them, and re-layouts: 3.84 us -> 18 us
  waiting for transfers between devices: 86 us -> 93.9 us
  starting transfers between devices: 46.2 us -> 42.4 us
    ppermute x10, waiting for transfers between devices: 32.5 us -> 53.8 us  [up(): return lax.ppermute(a, axis, ring(lax.axis_size(axis), 1))]
    dynamic_update_slice x0 -> x35, local copies, waits for them, and re-layouts: none -> 12.4 us  [put(): return lax.dynamic_update_slice(stack, piece[None], at)]
    ppermute x10, waiting for transfers between devices: 38.8 us -> 31.3 us  [down(): return lax.ppermute(a, axis, ring(lax.axis_size(axis), -1))]
    ppermute x1, waiting for transfers between devices: 4.88 us -> 0.01 us  [per_device(): c[0], c[4] = ((c[0], 0), (lax.ppermute(b[4], 'xh', ring(2, 1)), 0))]
    ppermute x2, waiting for transfers between devices: 9.71 us -> 5.96 us  [crossed(): return lax.ppermute(a, ('y', 'core'), pairs)]
    ppermute x1, waiting for transfers between devices: 0.01 us -> 2.78 us  [per_device(): near = lax.ppermute(mine, 'xl', ring(2, 1))]
    pallas_call x2 -> x5, Pallas kernels: 15.3 us -> 14.7 us  [the longest x4 14.7 us: call(): pl.pallas_call(kernel, out_shape=jax.ShapeDtypeStruct((rows, width), jnp....]
  transfers between devices with their start and end apart: 30 -> 30, of which waited for: 16 -> 11; matrix products, arithmetic and copies ran while one was open for 2% -> 10% of each run, Pallas kernels for 5% -> 7%
where the time goes in v1:
time: 172 us; the launch traced here: 171 us
  waiting for transfers between devices  93.9 us (55%)
  starting transfers between devices  42.4 us (25%)
  local copies, waits for them, and re-layouts  18 us (10%)
  Pallas kernels  14.7 us (9%)
  other arithmetic  1.78 us (1%)
    ppermute x10, waiting for transfers between devices, up(): return lax.ppermute(a, axis, ring(lax.axis_size(axis), 1))  53.8 us
    ppermute x10, waiting for transfers between devices, down(): return lax.ppermute(a, axis, ring(lax.axis_size(axis), -1))  31.3 us
    ppermute x10, starting transfers between devices, down(): return lax.ppermute(a, axis, ring(lax.axis_size(axis), -1))  19.6 us
    pallas_call x4, Pallas kernels, call(): pl.pallas_call(kernel, out_shape=jax.ShapeDtypeStruct((rows, width), jnp....  14.7 us
    dynamic_update_slice x35, local copies, waits for them, and re-layouts, put(): return lax.dynamic_update_slice(stack, piece[None], at)  12.4 us
    ppermute x2, waiting for transfers between devices, crossed(): return lax.ppermute(a, ('y', 'core'), pairs)  5.96 us
    ppermute x2, starting transfers between devices, crossed(): return lax.ppermute(a, ('y', 'core'), pairs)  5.43 us
    ppermute x3, starting transfers between devices, per_device(): pair = lax.ppermute(jnp.concatenate([b[-d], b[d]], 0), 'xh', ring(2, 1))  5.13 us
  transfers between devices with their start and end apart: 30, of which 11 were waited for; matrix products, arithmetic and copies ran while one was open for 10% of the time, Pallas kernels for 7%

profile of v1, /device:TPU:1, one launch (start us, length us, event | category | flops | bytes accessed | tf_op | source)
XLA Modules:
  0.0 171.3 jit_solution(1801810420234273990)
XLA Ops:
  0.0 1.1 constant_dynamic-slice_fusion
  1.1 6.5 %collective-permute-start.1 = (bf16[352,512]{1,0:T(8,128)(2,1)S(1)}, bf16[352,512]{1,0:T(8,128)(2,1)S(1)}, u32[]{:S(2)}, u32[]{:S(2)}) collective-permute-start(bf16[352,512]{1,0:T(8,128)(2,1)S(1)} %constant_dynamic-slice_fusion), channel_id=1, source_target_pairs={{0,28},{4,0},{8,4},{12,8},{16,12},{20,16},{24,20},{28,24},{1,29},{... | collective-permute-start | bytes 1081352 | tf_op jit(solution)/shard_map/ppermute | solution.py:132
  7.6 2.2 %fusion.6 = (bf16[512,512]{1,0:T(8,128)(2,1)}, bf16[512,512]{1,0:T(8,128)(2,1)}) fusion(bf16[1024,1024]{1,0:T(8,128)(2,1)} %param.3, s32[]{:T(128)S(6)} %select_n.33, s32[]{:T(128)S(6)} %select_n.34, s32[]{:T(128)S(6)} %select_n.31), kind=kLoop, calls=%fused_computation.49 | loop fusion | bytes 2097164 | tf_op jit(solution)/shard_map/dynamic_slice | solution.py:141
  9.8 1.0 collective-permute-start.10
  10.8 2.0 %bitcast_dynamic-update-slice_fusion.18 = (bf16[8,512,1024]{2,1,0:T(8,128)(2,1)}, bf16[512,512]{1,0:T(8,128)(2,1)S(1)}) fusion(bf16[8,512,1024]{2,1,0:T(8,128)(2,1)} %get-tuple-element.10, s32[]{:T(128)S(6)} %select_n.32, bf16[1024,1024]{1,0:T(8,128)(2,1)} %param.3, s32[]{:T(128)S(6)} %select_n.30, s32[]{:T(128)S(6)} %select_n.31), kind=kLoop, calls=%fused_computation.23 | loop fusion | bytes 1572876 | tf_op jit(solution)/shard_map/dynamic_update_slice | solution.py:184
  12.8 1.2 collective-permute-start.11
  14.0 2.0 %collective-permute-start.12 = (bf16[512,512]{1,0:T(8,128)(2,1)}, bf16[512,512]{1,0:T(8,128)(2,1)}, u32[]{:S(2)}, u32[]{:S(2)}) collective-permute-start(bf16[512,512]{1,0:T(8,128)(2,1)} %get-tuple-element.15), channel_id=1, source_target_pairs={{0,35},{1,34},{2,33},{3,32},{32,3},{33,2},{34,1},{35,0},{4,39},{5,... | collective-permute-start | bytes 1572872 | tf_op jit(solution)/shard_map/ppermute | solution.py:167
  16.0 1.9 %bitcast_dynamic-update-slice_fusion.12 = bf16[5,1280,512]{2,1,0:T(8,128)(2,1)} fusion(bf16[5,1280,512]{2,1,0:T(8,128)(2,1)} %get-tuple-element.9, bf16[1280,512]{1,0:T(8,128)(2,1)} %param.2), kind=kLoop, calls=%fused_computation.17 | loop fusion | bytes 1179648 | tf_op jit(solution)/shard_map/dynamic_update_slice | solution.py:184
  17.9 1.8 %bitcast_dynamic-update-slice_fusion.28 = bf16[5,1280,512]{2,1,0:T(8,128)(2,1)} fusion(bf16[5,1280,512]{2,1,0:T(8,128)(2,1)} %bitcast_dynamic-update-slice_fusion.12, s32[]{:T(128)S(6)} %select_n.28, bf16[1280,512]{1,0:T(8,128)(2,1)} %param.2), kind=kLoop, calls=%fused_computation.45 | loop fusion | bytes 720900 | tf_op jit(solution)/shard_map/dynamic_update_slice | solution.py:184
  19.8 0.8 bitcast_dynamic-update-slice_fusion.27
  20.5 1.2 collective-permute-start.13
  21.8 1.7 %collective-permute-start.14 = (bf16[512,512]{1,0:T(8,128)(2,1)}, bf16[512,512]{1,0:T(8,128)(2,1)S(1)}, u32[]{:S(2)}, u32[]{:S(2)}) collective-permute-start(bf16[512,512]{1,0:T(8,128)(2,1)} %get-tuple-element.16), channel_id=1, source_target_pairs={{0,66},{2,64},{64,130},{66,128},{128,194},{130,192},{192,2},{194,0... | collective-permute-start | bytes 1572872 | tf_op jit(solution)/shard_map/ppermute | solution.py:138
  23.6 2.8 %collective-permute-done.11 = bf16[512,512]{1,0:T(8,128)(2,1)} collective-permute-done((bf16[512,512]{1,0:T(8,128)(2,1)S(1)}, bf16[512,512]{1,0:T(8,128)(2,1)}, u32[]{:S(2)}, u32[]{:S(2)}) %collective-permute-start.11) | collective-permute-done | bytes 524320 | tf_op jit(solution)/shard_map/ppermute | solution.py:166
  26.4 2.7 %collective-permute-start.16 = (bf16[512,512]{1,0:T(8,128)(2,1)S(1)}, bf16[512,512]{1,0:T(8,128)(2,1)S(1)}, u32[]{:S(2)}, u32[]{:S(2)}) collective-permute-start(bf16[512,512]{1,0:T(8,128)(2,1)S(1)} %get-tuple-element.14), channel_id=1, source_target_pairs={{0,192},{64,0},{128,64},{192,128},{1,193},{65,1},{129,65},{193,129... | collective-permute-start | bytes 1572872 | tf_op jit(solution)/shard_map/ppermute | solution.py:132
  29.1 1.1 constant_dynamic-update-slice_fusion.1
  30.2 3.0 %collective-permute-start = (bf16[576,512]{1,0:T(8,128)(2,1)S(1)}, bf16[576,512]{1,0:T(8,128)(2,1)S(1)}, u32[]{:S(2)}, u32[]{:S(2)}) collective-permute-start(bf16[576,512]{1,0:T(8,128)(2,1)S(1)} %slice.21), channel_id=1, source_target_pairs={{0,28},{4,0},{8,4},{12,8},{16,12},{20,16},{24,20},{28,24},{1,29},{... | collective-permute-start | bytes 1769480 | tf_op jit(solution)/shard_map/ppermute | solution.py:132
  33.2 1.1 constant_dynamic-update-slice_fusion
  34.3 2.8 %collective-permute-start.3 = (bf16[704,512]{1,0:T(8,128)(2,1)S(1)}, bf16[704,512]{1,0:T(8,128)(2,1)S(1)}, u32[]{:S(2)}, u32[]{:S(2)}) collective-permute-start(bf16[704,512]{1,0:T(8,128)(2,1)S(1)} %pad_maximum_fusion.1), channel_id=1, source_target_pairs={{0,1},{1,0},{2,3},{3,2},{4,5},{5,4},{6,7},{7,6},{8,9},{9,8},{10,11... | collective-permute-start | bytes 2162696 | tf_op jit(solution)/shard_map/ppermute | solution.py:159
  37.2 1.9 %bitcast_dynamic-update-slice_fusion.17 = bf16[8,512,1024]{2,1,0:T(8,128)(2,1)} fusion(bf16[8,512,1024]{2,1,0:T(8,128)(2,1)} %get-tuple-element.13, s32[]{:T(128)S(6)} %select_n.32, bf16[512,512]{1,0:T(8,128)(2,1)} %collective-permute-done.10), kind=kLoop, calls=%fused_computation.22 | loop fusion | bytes 1048580 | tf_op jit(solution)/shard_map/dynamic_update_slice | solution.py:184
  39.1 1.0 bitcast_dynamic-update-slice_fusion.4
  40.1 0.9 bitcast_dynamic-update-slice_fusion.16
  41.0 6.0 %collective-permute-done.14 = bf16[512,512]{1,0:T(8,128)(2,1)S(1)} collective-permute-done((bf16[512,512]{1,0:T(8,128)(2,1)}, bf16[512,512]{1,0:T(8,128)(2,1)S(1)}, u32[]{:S(2)}, u32[]{:S(2)}) %collective-permute-start.14) | collective-permute-done | bytes 524320 | tf_op jit(solution)/shard_map/ppermute | solution.py:138
  47.0 0.8 bitcast_dynamic-update-slice_fusion.15
  47.8 0.1 pad_maximum_fusion
  48.0 3.1 %collective-permute-start.4 = (bf16[576,512]{1,0:T(8,128)(2,1)S(1)}, bf16[576,512]{1,0:T(8,128)(2,1)S(1)}, u32[]{:S(2)}, u32[]{:S(2)}) collective-permute-start(bf16[576,512]{1,0:T(8,128)(2,1)S(1)} %collective-permute-done), channel_id=1, source_target_pairs={{0,28},{4,0},{8,4},{12,8},{16,12},{20,16},{24,20},{28,24},{1,29},{... | collective-permute-start | bytes 1769480 | tf_op jit(solution)/shard_map/ppermute | solution.py:132
  51.2 1.3 collective-permute-done.5
  52.5 3.4 %collective-permute-start.20 = (bf16[352,512]{1,0:T(8,128)(2,1)S(1)}, bf16[352,512]{1,0:T(8,128)(2,1)S(1)}, u32[]{:S(2)}, u32[]{:S(2)}) collective-permute-start(bf16[352,512]{1,0:T(8,128)(2,1)S(1)} %collective-permute-done.5), channel_id=1, source_target_pairs={{0,28},{4,0},{8,4},{12,8},{16,12},{20,16},{24,20},{28,24},{1,29},{... | collective-permute-start | bytes 1081352 | tf_op jit(solution)/shard_map/ppermute | solution.py:132
  55.9 2.9 %collective-permute-done.6 = bf16[352,512]{1,0:T(8,128)(2,1)S(1)} collective-permute-done((bf16[352,512]{1,0:T(8,128)(2,1)S(1)}, bf16[352,512]{1,0:T(8,128)(2,1)S(1)}, u32[]{:S(2)}, u32[]{:S(2)}) %collective-permute-start.6) | collective-permute-done | bytes 360480 | tf_op jit(solution)/shard_map/ppermute | solution.py:129
  58.9 0.8 collective-permute-start.7
  59.7 13.2 %collective-permute-done.20 = bf16[352,512]{1,0:T(8,128)(2,1)S(1)} collective-permute-done((bf16[352,512]{1,0:T(8,128)(2,1)S(1)}, bf16[352,512]{1,0:T(8,128)(2,1)S(1)}, u32[]{:S(2)}, u32[]{:S(2)}) %collective-permute-start.20) | collective-permute-done | bytes 360480 | tf_op jit(solution)/shard_map/ppermute | solution.py:132
  72.9 3.7 %collective-permute-start.17 = (bf16[512,512]{1,0:T(8,128)(2,1)}, bf16[512,512]{1,0:T(8,128)(2,1)S(1)}, u32[]{:S(2)}, u32[]{:S(2)}) collective-permute-start(bf16[512,512]{1,0:T(8,128)(2,1)} %get-tuple-element.16), channel_id=1, source_target_pairs={{0,194},{2,192},{64,2},{66,0},{128,66},{130,64},{192,130},{194,128... | collective-permute-start | bytes 1572872 | tf_op jit(solution)/shard_map/ppermute | solution.py:138
  76.8 16.6 %collective-permute-done.8 = bf16[576,512]{1,0:T(8,128)(2,1)S(1)} collective-permute-done((bf16[576,512]{1,0:T(8,128)(2,1)S(1)}, bf16[576,512]{1,0:T(8,128)(2,1)S(1)}, u32[]{:S(2)}, u32[]{:S(2)}) %collective-permute-start.8) | collective-permute-done | bytes 589856 | tf_op jit(solution)/shard_map/ppermute | solution.py:129
  93.4 0.6 collective-permute-start.18
  94.2 15.3 %collective-permute-done.9 = bf16[576,512]{1,0:T(8,128)(2,1)S(1)} collective-permute-done((bf16[576,512]{1,0:T(8,128)(2,1)S(1)}, bf16[576,512]{1,0:T(8,128)(2,1)S(1)}, u32[]{:S(2)}, u32[]{:S(2)}) %collective-permute-start.9) | collective-permute-done | bytes 589856 | tf_op jit(solution)/shard_map/ppermute | solution.py:129
  109.4 1.3 collective-permute-start.27
  110.9 1.5 collective-permute-start.22
  112.9 7.8 %collective-permute-done.25 = bf16[352,512]{1,0:T(8,128)(2,1)S(1)} collective-permute-done((bf16[352,512]{1,0:T(8,128)(2,1)S(1)}, bf16[352,512]{1,0:T(8,128)(2,1)S(1)}, u32[]{:S(2)}, u32[]{:S(2)}) %collective-permute-start.25) | collective-permute-done | bytes 360480 | tf_op jit(solution)/shard_map/ppermute | solution.py:132
  120.7 1.8 %collective-permute-start.26 = (bf16[352,512]{1,0:T(8,128)(2,1)S(1)}, bf16[352,512]{1,0:T(8,128)(2,1)S(1)}, u32[]{:S(2)}, u32[]{:S(2)}) collective-permute-start(bf16[352,512]{1,0:T(8,128)(2,1)S(1)} %collective-permute-done.25), channel_id=1, source_target_pairs={{0,1},{1,0},{2,3},{3,2},{4,5},{5,4},{6,7},{7,6},{8,9},{9,8},{10,11... | collective-permute-start | bytes 1081352 | tf_op jit(solution)/shard_map/ppermute | solution.py:161
  122.6 4.6 %shard_map.30.total_ref = f32[1280,512]{1,0:T(8,128)S(1)} custom-call(bf16[5,1280,512]{2,1,0:T(8,128)(2,1)S(1)} %fusion.2.t_ref.tn_ref, bf16[8,512,1024]{2,1,0:T(8,128)(2,1)S(1)} %bitcast_dynamic-update-slice_fusion.2.w_ref.wn_ref), custom_call_target="tpu_custom_call" | custom-call | flops 3355443200 | bytes 14417920 | tf_op jit(solution)/shard_map/pallas_call | solution.py:46
  127.2 6.6 %collective-permute-done.27 = bf16[512,1024]{1,0:T(8,128)(2,1)S(1)} collective-permute-done((bf16[512,1024]{1,0:T(8,128)(2,1)S(1)}, bf16[512,1024]{1,0:T(8,128)(2,1)S(1)}, u32[]{:S(2)}, u32[]{:S(2)}) %collective-permute-start.27) | collective-permute-done | bytes 1048608 | tf_op jit(solution)/shard_map/ppermute | solution.py:129
  134.0 0.3 collective-permute-start.24
  134.6 12.4 %collective-permute-done.24 = bf16[576,512]{1,0:T(8,128)(2,1)S(1)} collective-permute-done((bf16[576,512]{1,0:T(8,128)(2,1)S(1)}, bf16[576,512]{1,0:T(8,128)(2,1)S(1)}, u32[]{:S(2)}, u32[]{:S(2)}) %collective-permute-start.24) | collective-permute-done | bytes 589856 | tf_op jit(solution)/shard_map/ppermute | solution.py:129
  147.1 9.0 %collective-permute-done.28 = bf16[512,1024]{1,0:T(8,128)(2,1)S(1)} collective-permute-done((bf16[512,1024]{1,0:T(8,128)(2,1)S(1)}, bf16[512,1024]{1,0:T(8,128)(2,1)S(1)}, u32[]{:S(2)}, u32[]{:S(2)}) %collective-permute-start.28) | collective-permute-done | bytes 1048608 | tf_op jit(solution)/shard_map/ppermute | solution.py:132
  156.3 2.8 %shard_map.31 = f32[1280,512]{1,0:T(8,128)S(1)} custom-call(f32[1280,512]{1,0:T(8,128)S(1)} %shard_map.30.total_ref, bf16[5,1280,512]{2,1,0:T(8,128)(2,1)S(1)} %fusion.2.t_ref.tn_ref, bf16[3,1280,512]{2,1,0:T(8,128)(2,1)S(1)} %bitcast_dynamic-update-slice_fusion.19.tl_ref, ...), custom_call_target="tpu_custom_call", output_to_operand_aliasing={{}: (0, {})} | custom-call | flops 2013265920 | bytes 10747904 | tf_op jit(solution)/shard_map/pallas_call | solution.py:46
  159.1 3.3 %collective-permute-start.29 = (f32[1280,512]{1,0:T(8,128)S(1)}, f32[1280,512]{1,0:T(8,128)S(1)}, u32[]{:S(2)}, u32[]{:S(2)}) collective-permute-start(f32[1280,512]{1,0:T(8,128)S(1)} %shard_map.31), channel_id=1, source_target_pairs={{0,2},{2,0},{1,3},{3,1},{4,6},{6,4},{5,7},{7,5},{8,10},{10,8},{9,1... | collective-permute-start | bytes 7864328 | tf_op jit(solution)/shard_map/ppermute | solution.py:209
  162.4 4.5 %shard_map.28.total_ref = f32[1280,512]{1,0:T(8,128)S(1)} custom-call(bf16[5,1280,512]{2,1,0:T(8,128)(2,1)S(1)} %fusion.2.t_ref.tn_ref, bf16[8,512,1024]{2,1,0:T(8,128)(2,1)S(1)} %bitcast_dynamic-update-slice_fusion.2.w_ref.wn_ref), custom_call_target="tpu_custom_call" | custom-call | flops 3355443200 | bytes 14417920 | tf_op jit(solution)/shard_map/pallas_call | solution.py:46
  167.0 2.8 %shard_map.29 = f32[1280,512]{1,0:T(8,128)S(1)} custom-call(f32[1280,512]{1,0:T(8,128)S(1)} %shard_map.28.total_ref, bf16[5,1280,512]{2,1,0:T(8,128)(2,1)S(1)} %fusion.2.t_ref.tn_ref, bf16[3,1280,512]{2,1,0:T(8,128)(2,1)S(1)} %bitcast_dynamic-update-slice_fusion.19.tl_ref, ...), custom_call_target="tpu_custom_call", output_to_operand_aliasing={{}: (0, {})} | custom-call | flops 2013265920 | bytes 10747904 | tf_op jit(solution)/shard_map/pallas_call | solution.py:46
  169.8 1.5 add_convert_fusion
  (75 shorter events, 1.8 us)
Async XLA Ops:
  0.0 19.7 %copy-start.3 = (bf16[1280,512]{1,0:T(8,128)(2,1)S(1)}, bf16[1280,512]{1,0:T(8,128)(2,1)}, u32[]{:S(2)}) copy-start(bf16[1280,512]{1,0:T(8,128)(2,1)} %param.2) | copy-start | bytes 3932164
  1.1 19.4 %collective-permute-start.1 = (bf16[352,512]{1,0:T(8,128)(2,1)S(1)}, bf16[352,512]{1,0:T(8,128)(2,1)S(1)}, u32[]{:S(2)}, u32[]{:S(2)}) collective-permute-start(bf16[352,512]{1,0:T(8,128)(2,1)S(1)} %constant_dynamic-slice_fusion), channel_id=1, source_target_pairs={{0,28},{4,0},{8,4},{12,8},{16,12},{20,16},{24,20},{28,24},{1,29},{... | collective-permute-start | bytes 1081352 | tf_op jit(solution)/shard_map/ppermute | solution.py:132
  7.6 14.2 %collective-permute-start.2 = (bf16[352,512]{1,0:T(8,128)(2,1)S(1)}, bf16[352,512]{1,0:T(8,128)(2,1)S(1)}, u32[]{:S(2)}, u32[]{:S(2)}) collective-permute-start(bf16[352,512]{1,0:T(8,128)(2,1)S(1)} %constant_dynamic-slice_fusion), channel_id=1, source_target_pairs={{0,4},{4,8},{8,12},{12,16},{16,20},{20,24},{24,28},{28,0},{1,5},{5... | collective-permute-start | bytes 1081352 | tf_op jit(solution)/shard_map/ppermute | solution.py:129
  9.8 24.5 %collective-permute-start.10 = (bf16[512,512]{1,0:T(8,128)(2,1)}, bf16[512,512]{1,0:T(8,128)(2,1)}, u32[]{:S(2)}, u32[]{:S(2)}) collective-permute-start(bf16[512,512]{1,0:T(8,128)(2,1)} %get-tuple-element.16), channel_id=1, source_target_pairs={{0,2},{2,0},{1,3},{3,1},{4,6},{6,4},{5,7},{7,5},{8,10},{10,8},{9,1... | collective-permute-start | bytes 1572872 | tf_op jit(solution)/shard_map/ppermute | solution.py:168
  12.8 13.6 %collective-permute-start.11 = (bf16[512,512]{1,0:T(8,128)(2,1)S(1)}, bf16[512,512]{1,0:T(8,128)(2,1)}, u32[]{:S(2)}, u32[]{:S(2)}) collective-permute-start(bf16[512,512]{1,0:T(8,128)(2,1)S(1)} %get-tuple-element.14), channel_id=1, source_target_pairs={{0,32},{32,0},{1,33},{33,1},{2,34},{34,2},{3,35},{35,3},{4,36},{36... | collective-permute-start | bytes 1572872 | tf_op jit(solution)/shard_map/ppermute | solution.py:166
  14.0 16.2 %collective-permute-start.12 = (bf16[512,512]{1,0:T(8,128)(2,1)}, bf16[512,512]{1,0:T(8,128)(2,1)}, u32[]{:S(2)}, u32[]{:S(2)}) collective-permute-start(bf16[512,512]{1,0:T(8,128)(2,1)} %get-tuple-element.15), channel_id=1, source_target_pairs={{0,35},{1,34},{2,33},{3,32},{32,3},{33,2},{34,1},{35,0},{4,39},{5,... | collective-permute-start | bytes 1572872 | tf_op jit(solution)/shard_map/ppermute | solution.py:167
  20.5 30.6 %copy-start = (bf16[5,1280,512]{2,1,0:T(8,128)(2,1)S(1)}, bf16[5,1280,512]{2,1,0:T(8,128)(2,1)}, u32[]{:S(2)}) copy-start(bf16[5,1280,512]{2,1,0:T(8,128)(2,1)} %bitcast_dynamic-update-slice_fusion.27) | copy-start | bytes 19660804
  20.5 19.6 %collective-permute-start.13 = (bf16[512,512]{1,0:T(8,128)(2,1)S(1)}, bf16[512,512]{1,0:T(8,128)(2,1)S(1)}, u32[]{:S(2)}, u32[]{:S(2)}) collective-permute-start(bf16[512,512]{1,0:T(8,128)(2,1)S(1)} %get-tuple-element.14), channel_id=1, source_target_pairs={{0,64},{64,128},{128,192},{192,0},{1,65},{65,129},{129,193},{193,1... | collective-permute-start | bytes 1572872 | tf_op jit(solution)/shard_map/ppermute | solution.py:129
  21.8 25.2 %collective-permute-start.14 = (bf16[512,512]{1,0:T(8,128)(2,1)}, bf16[512,512]{1,0:T(8,128)(2,1)S(1)}, u32[]{:S(2)}, u32[]{:S(2)}) collective-permute-start(bf16[512,512]{1,0:T(8,128)(2,1)} %get-tuple-element.16), channel_id=1, source_target_pairs={{0,66},{2,64},{64,130},{66,128},{128,194},{130,192},{192,2},{194,0... | collective-permute-start | bytes 1572872 | tf_op jit(solution)/shard_map/ppermute | solution.py:138
  26.4 86.1 %collective-permute-start.16 = (bf16[512,512]{1,0:T(8,128)(2,1)S(1)}, bf16[512,512]{1,0:T(8,128)(2,1)S(1)}, u32[]{:S(2)}, u32[]{:S(2)}) collective-permute-start(bf16[512,512]{1,0:T(8,128)(2,1)S(1)} %get-tuple-element.14), channel_id=1, source_target_pairs={{0,192},{64,0},{128,64},{192,128},{1,193},{65,1},{129,65},{193,129... | collective-permute-start | bytes 1572872 | tf_op jit(solution)/shard_map/ppermute | solution.py:132
  30.2 17.8 %collective-permute-start = (bf16[576,512]{1,0:T(8,128)(2,1)S(1)}, bf16[576,512]{1,0:T(8,128)(2,1)S(1)}, u32[]{:S(2)}, u32[]{:S(2)}) collective-permute-start(bf16[576,512]{1,0:T(8,128)(2,1)S(1)} %slice.21), channel_id=1, source_target_pairs={{0,28},{4,0},{8,4},{12,8},{16,12},{20,16},{24,20},{28,24},{1,29},{... | collective-permute-start | bytes 1769480 | tf_op jit(solution)/shard_map/ppermute | solution.py:132
  34.3 24.5 %collective-permute-start.3 = (bf16[704,512]{1,0:T(8,128)(2,1)S(1)}, bf16[704,512]{1,0:T(8,128)(2,1)S(1)}, u32[]{:S(2)}, u32[]{:S(2)}) collective-permute-start(bf16[704,512]{1,0:T(8,128)(2,1)S(1)} %pad_maximum_fusion.1), channel_id=1, source_target_pairs={{0,1},{1,0},{2,3},{3,2},{4,5},{5,4},{6,7},{7,6},{8,9},{9,8},{10,11... | collective-permute-start | bytes 2162696 | tf_op jit(solution)/shard_map/ppermute | solution.py:159
  40.1 12.4 %collective-permute-start.5 = (bf16[352,512]{1,0:T(8,128)(2,1)S(1)}, bf16[352,512]{1,0:T(8,128)(2,1)S(1)}, u32[]{:S(2)}, u32[]{:S(2)}) collective-permute-start(bf16[352,512]{1,0:T(8,128)(2,1)S(1)} %collective-permute-done.1), channel_id=1, source_target_pairs={{0,28},{4,0},{8,4},{12,8},{16,12},{20,16},{24,20},{28,24},{1,29},{... | collective-permute-start | bytes 1081352 | tf_op jit(solution)/shard_map/ppermute | solution.py:132
  47.0 11.8 %collective-permute-start.6 = (bf16[352,512]{1,0:T(8,128)(2,1)S(1)}, bf16[352,512]{1,0:T(8,128)(2,1)S(1)}, u32[]{:S(2)}, u32[]{:S(2)}) collective-permute-start(bf16[352,512]{1,0:T(8,128)(2,1)S(1)} %collective-permute-done.2), channel_id=1, source_target_pairs={{0,4},{4,8},{8,12},{12,16},{16,20},{20,24},{24,28},{28,0},{1,5},{5... | collective-permute-start | bytes 1081352 | tf_op jit(solution)/shard_map/ppermute | solution.py:129
  47.8 64.6 %slice-start = ((s8[8388608]{0:T(1024)(128)(4,1)}), s8[4194304]{0:T(1024)(128)(4,1)S(1)}, s32[]{:S(2)}) async-start(s8[8388608]{0:T(1024)(128)(4,1)} %bitcast.82), calls=%async_computation | async-start | bytes 8388608
  48.0 28.6 %collective-permute-start.4 = (bf16[576,512]{1,0:T(8,128)(2,1)S(1)}, bf16[576,512]{1,0:T(8,128)(2,1)S(1)}, u32[]{:S(2)}, u32[]{:S(2)}) collective-permute-start(bf16[576,512]{1,0:T(8,128)(2,1)S(1)} %collective-permute-done), channel_id=1, source_target_pairs={{0,28},{4,0},{8,4},{12,8},{16,12},{20,16},{24,20},{28,24},{1,29},{... | collective-permute-start | bytes 1769480 | tf_op jit(solution)/shard_map/ppermute | solution.py:132
  52.5 20.4 %collective-permute-start.20 = (bf16[352,512]{1,0:T(8,128)(2,1)S(1)}, bf16[352,512]{1,0:T(8,128)(2,1)S(1)}, u32[]{:S(2)}, u32[]{:S(2)}) collective-permute-start(bf16[352,512]{1,0:T(8,128)(2,1)S(1)} %collective-permute-done.5), channel_id=1, source_target_pairs={{0,28},{4,0},{8,4},{12,8},{16,12},{20,16},{24,20},{28,24},{1,29},{... | collective-permute-start | bytes 1081352 | tf_op jit(solution)/shard_map/ppermute | solution.py:132
  58.8 17.8 %collective-permute-start.21 = (bf16[352,512]{1,0:T(8,128)(2,1)S(1)}, bf16[352,512]{1,0:T(8,128)(2,1)S(1)}, u32[]{:S(2)}, u32[]{:S(2)}) collective-permute-start(bf16[352,512]{1,0:T(8,128)(2,1)S(1)} %collective-permute-done.6), channel_id=1, source_target_pairs={{0,4},{4,8},{8,12},{12,16},{16,20},{20,24},{24,28},{28,0},{1,5},{5... | collective-permute-start | bytes 1081352 | tf_op jit(solution)/shard_map/ppermute | solution.py:129
  58.9 35.2 %collective-permute-start.7 = (bf16[704,512]{1,0:T(8,128)(2,1)S(1)}, bf16[704,512]{1,0:T(8,128)(2,1)S(1)}, u32[]{:S(2)}, u32[]{:S(2)}) collective-permute-start(bf16[704,512]{1,0:T(8,128)(2,1)S(1)} %pad_maximum_fusion.2), channel_id=1, source_target_pairs={{0,1},{1,0},{2,3},{3,2},{4,5},{5,4},{6,7},{7,6},{8,9},{9,8},{10,11... | collective-permute-start | bytes 2162696 | tf_op jit(solution)/shard_map/ppermute | solution.py:159
  72.9 39.9 %collective-permute-start.17 = (bf16[512,512]{1,0:T(8,128)(2,1)}, bf16[512,512]{1,0:T(8,128)(2,1)S(1)}, u32[]{:S(2)}, u32[]{:S(2)}) collective-permute-start(bf16[512,512]{1,0:T(8,128)(2,1)} %get-tuple-element.16), channel_id=1, source_target_pairs={{0,194},{2,192},{64,2},{66,0},{128,66},{130,64},{192,130},{194,128... | collective-permute-start | bytes 1572872 | tf_op jit(solution)/shard_map/ppermute | solution.py:138
  76.5 16.8 %collective-permute-start.8 = (bf16[576,512]{1,0:T(8,128)(2,1)S(1)}, bf16[576,512]{1,0:T(8,128)(2,1)S(1)}, u32[]{:S(2)}, u32[]{:S(2)}) collective-permute-start(bf16[576,512]{1,0:T(8,128)(2,1)S(1)} %slice.21), channel_id=1, source_target_pairs={{0,4},{4,8},{8,12},{12,16},{16,20},{20,24},{24,28},{28,0},{1,5},{5... | collective-permute-start | bytes 1769480 | tf_op jit(solution)/shard_map/ppermute | solution.py:129
  76.6 35.8 %slice-start.1 = ((s8[8388608]{0:T(1024)(128)(4,1)}), s8[4194304]{0:T(1024)(128)(4,1)S(1)}, s32[]{:S(2)}) async-start(s8[8388608]{0:T(1024)(128)(4,1)} %bitcast.82), calls=%async_computation.1 | async-start | bytes 8388608
  76.6 34.2 %collective-permute-start.15 = (bf16[512,1024]{1,0:T(8,128)(2,1)S(1)}, bf16[512,1024]{1,0:T(8,128)(2,1)S(1)}, u32[]{:S(2)}, u32[]{:S(2)}) collective-permute-start(bf16[512,1024]{1,0:T(8,128)(2,1)S(1)} %constant_dynamic-update-slice_fusion), channel_id=1, source_target_pairs={{0,64},{64,128},{128,192},{192,0},{1,65},{65,129},{129,193},{193,1... | collective-permute-start | bytes 3145736 | tf_op jit(solution)/shard_map/ppermute | solution.py:129
  93.4 27.3 %collective-permute-start.18 = (bf16[512,1024]{1,0:T(8,128)(2,1)S(1)}, bf16[512,1024]{1,0:T(8,128)(2,1)S(1)}, u32[]{:S(2)}, u32[]{:S(2)}) collective-permute-start(bf16[512,1024]{1,0:T(8,128)(2,1)S(1)} %constant_dynamic-update-slice_fusion), channel_id=1, source_target_pairs={{0,192},{64,0},{128,64},{192,128},{1,193},{65,1},{129,65},{193,129... | collective-permute-start | bytes 3145736 | tf_op jit(solution)/shard_map/ppermute | solution.py:132
  94.0 15.4 %collective-permute-start.9 = (bf16[576,512]{1,0:T(8,128)(2,1)S(1)}, bf16[576,512]{1,0:T(8,128)(2,1)S(1)}, u32[]{:S(2)}, u32[]{:S(2)}) collective-permute-start(bf16[576,512]{1,0:T(8,128)(2,1)S(1)} %collective-permute-done.8), channel_id=1, source_target_pairs={{0,4},{4,8},{8,12},{12,16},{16,20},{20,24},{24,28},{28,0},{1,5},{5... | collective-permute-start | bytes 1769480 | tf_op jit(solution)/shard_map/ppermute | solution.py:129
  109.4 24.4 %collective-permute-start.27 = (bf16[512,1024]{1,0:T(8,128)(2,1)S(1)}, bf16[512,1024]{1,0:T(8,128)(2,1)S(1)}, u32[]{:S(2)}, u32[]{:S(2)}) collective-permute-start(bf16[512,1024]{1,0:T(8,128)(2,1)S(1)} %pad_maximum_fusion), channel_id=1, source_target_pairs={{0,64},{64,128},{128,192},{192,0},{1,65},{65,129},{129,193},{193,1... | collective-permute-start | bytes 3145736 | tf_op jit(solution)/shard_map/ppermute | solution.py:129
  110.9 23.5 %collective-permute-start.22 = (bf16[704,512]{1,0:T(8,128)(2,1)S(1)}, bf16[704,512]{1,0:T(8,128)(2,1)S(1)}, u32[]{:S(2)}, u32[]{:S(2)}) collective-permute-start(bf16[704,512]{1,0:T(8,128)(2,1)S(1)} %pad_maximum_fusion.3), channel_id=1, source_target_pairs={{0,1},{1,0},{2,3},{3,2},{4,5},{5,4},{6,7},{7,6},{8,9},{9,8},{10,11... | collective-permute-start | bytes 2162696 | tf_op jit(solution)/shard_map/ppermute | solution.py:159
  112.5 8.1 %collective-permute-start.25 = (bf16[352,512]{1,0:T(8,128)(2,1)S(1)}, bf16[352,512]{1,0:T(8,128)(2,1)S(1)}, u32[]{:S(2)}, u32[]{:S(2)}) collective-permute-start(bf16[352,512]{1,0:T(8,128)(2,1)S(1)} %collective-permute-done.20), channel_id=1, source_target_pairs={{0,28},{4,0},{8,4},{12,8},{16,12},{20,16},{24,20},{28,24},{1,29},{... | collective-permute-start | bytes 1081352 | tf_op jit(solution)/shard_map/ppermute | solution.py:132
  112.7 21.6 %collective-permute-start.19 = (bf16[576,512]{1,0:T(8,128)(2,1)S(1)}, bf16[576,512]{1,0:T(8,128)(2,1)S(1)}, u32[]{:S(2)}, u32[]{:S(2)}) collective-permute-start(bf16[576,512]{1,0:T(8,128)(2,1)S(1)} %collective-permute-done.4), channel_id=1, source_target_pairs={{0,28},{4,0},{8,4},{12,8},{16,12},{20,16},{24,20},{28,24},{1,29},{... | collective-permute-start | bytes 1769480 | tf_op jit(solution)/shard_map/ppermute | solution.py:132
  120.7 13.3 %collective-permute-start.23 = (bf16[576,512]{1,0:T(8,128)(2,1)S(1)}, bf16[576,512]{1,0:T(8,128)(2,1)S(1)}, u32[]{:S(2)}, u32[]{:S(2)}) collective-permute-start(bf16[576,512]{1,0:T(8,128)(2,1)S(1)} %collective-permute-done.9), channel_id=1, source_target_pairs={{0,4},{4,8},{8,12},{12,16},{16,20},{20,24},{24,28},{28,0},{1,5},{5... | collective-permute-start | bytes 1769480 | tf_op jit(solution)/shard_map/ppermute | solution.py:129
  120.7 26.4 %collective-permute-start.26 = (bf16[352,512]{1,0:T(8,128)(2,1)S(1)}, bf16[352,512]{1,0:T(8,128)(2,1)S(1)}, u32[]{:S(2)}, u32[]{:S(2)}) collective-permute-start(bf16[352,512]{1,0:T(8,128)(2,1)S(1)} %collective-permute-done.25), channel_id=1, source_target_pairs={{0,1},{1,0},{2,3},{3,2},{4,5},{5,4},{6,7},{7,6},{8,9},{9,8},{10,11... | collective-permute-start | bytes 1081352 | tf_op jit(solution)/shard_map/ppermute | solution.py:161
  122.6 11.2 %copy-start.2 = (bf16[2,512,1024]{2,1,0:T(8,128)(2,1)S(1)}, bf16[2,512,1024]{2,1,0:T(8,128)(2,1)}, u32[]{:S(2)}) copy-start(bf16[2,512,1024]{2,1,0:T(8,128)(2,1)} %get-tuple-element.12) | copy-start | bytes 6291460
  122.6 11.7 %copy-start.1 = (bf16[3,1280,512]{2,1,0:T(8,128)(2,1)S(1)}, bf16[3,1280,512]{2,1,0:T(8,128)(2,1)}, u32[]{:S(2)}) copy-start(bf16[3,1280,512]{2,1,0:T(8,128)(2,1)} %get-tuple-element.11) | copy-start | bytes 11796484
  133.8 22.3 %collective-permute-start.28 = (bf16[512,1024]{1,0:T(8,128)(2,1)S(1)}, bf16[512,1024]{1,0:T(8,128)(2,1)S(1)}, u32[]{:S(2)}, u32[]{:S(2)}) collective-permute-start(bf16[512,1024]{1,0:T(8,128)(2,1)S(1)} %collective-permute-done.18), channel_id=1, source_target_pairs={{0,192},{64,0},{128,64},{192,128},{1,193},{65,1},{129,65},{193,129... | collective-permute-start | bytes 3145736 | tf_op jit(solution)/shard_map/ppermute | solution.py:132
  134.0 13.0 %collective-permute-start.24 = (bf16[576,512]{1,0:T(8,128)(2,1)S(1)}, bf16[576,512]{1,0:T(8,128)(2,1)S(1)}, u32[]{:S(2)}, u32[]{:S(2)}) collective-permute-start(bf16[576,512]{1,0:T(8,128)(2,1)S(1)} %collective-permute-done.23), channel_id=1, source_target_pairs={{0,4},{4,8},{8,12},{12,16},{16,20},{20,24},{24,28},{28,0},{1,5},{5... | collective-permute-start | bytes 1769480 | tf_op jit(solution)/shard_map/ppermute | solution.py:129
  159.1 10.7 %collective-permute-start.29 = (f32[1280,512]{1,0:T(8,128)S(1)}, f32[1280,512]{1,0:T(8,128)S(1)}, u32[]{:S(2)}, u32[]{:S(2)}) collective-permute-start(f32[1280,512]{1,0:T(8,128)S(1)} %shard_map.31), channel_id=1, source_target_pairs={{0,2},{2,0},{1,3},{3,1},{4,6},{6,4},{5,7},{7,5},{8,10},{10,8},{9,1... | collective-permute-start | bytes 7864328 | tf_op jit(solution)/shard_map/ppermute | solution.py:209
